TPU v7x, 256 devices: a 2x2x32 block of a 4x8x32 slice. The times are simulated.
256 devices in a mesh: rep: 4 (over y, x), ep: 32 (over z), tp: 2 (over core).
Axes of the slice: x: 2, y: 2, z: 32, core: 2. Of those that a mesh axis runs over, the one named last changes fastest.
The devices are a block of a 4x8x32 slice.
Arguments:
- tokens: bfloat16 [8192, 3072], P(('rep', 'ep')), parts along dimension 0, may hold values from -6 to 6
- routes: int32 [8192, 2], P(('rep', 'ep')), parts along dimension 0, may hold values from 0 to 3, all different within a row; in each aligned block of 64 rows (0 to 63, 64 to 127, ...) at most 40 rows name the same one
- route_weight: float32 [8192, 2], P(('rep', 'ep')), parts along dimension 0, may hold values from 0.2 to 1
- gate_code: bfloat16 [3072, 32768], P(None, ('ep', 'tp')), may hold values from -0.109375 to 0.109375
- gate_scale: float32 [3072, 256], P(None, ('ep', 'tp')), may hold values from 0.5 to 2
- up_code: bfloat16 [3072, 32768], P(None, ('ep', 'tp')), may hold values from -0.109375 to 0.109375
- up_scale: float32 [3072, 256], P(None, ('ep', 'tp')), may hold values from 0.5 to 2
- down_code: bfloat16 [32768, 3072], P(('ep', 'tp')), may hold values from -0.0625 to 0.0625
- down_scale: float32 [32768, 24], P(('ep', 'tp')), may hold values from 0.5 to 2
Outputs:
- mixed: bfloat16 [8192, 3072], P(('rep', 'ep'), 'tp'), parts along dimension 0
There are 4 independent parts, one for each index of `rep`. A program takes and returns all parts, laid end to end along the dimension named above; an argument that names none is the same for every part. Nothing has to cross between parts.
Inputs may be any that keep to these rules, and one draw needn't show every extreme that they name: `routes`: among the 64 rows of one index of ep, no expert is named by more than 40 rows, a bound that some block reaches; a row names 2 different experts.
All inputs are finite; a program needn't handle non-finite values.
Results may differ from a plain program's by a relative error of at most 0.02.
Values may be sent and summed in bfloat16 or wider, within the bound.
A program may use at most 128 MiB of HBM per device.

v0:
```python
import jax
import jax.numpy as jnp
from jax import lax
from jax.sharding import PartitionSpec as P

EXPERTS = 4
TOP = 2
QB = 128
CAP = 40


def partner_2(block, axis, apart):
    count = lax.axis_size(axis)
    route = []
    for low in range(count):
        high = low | 1 << apart
        if high != low and high < count:
            route += [(low, high), (high, low)]
    return lax.ppermute(block, axis, route)


def cut_along(shard, dim, size):
    before, after = (shard.shape[:dim], shard.shape[dim + 1 :])
    return jnp.moveaxis(shard.reshape(*before, size, -1, *after), dim, 0)


def summed_on_arrival(shard, axis, dim):
    parts = cut_along(shard, dim, lax.axis_size(axis))
    arrived = lax.all_to_all(parts, axis, split_axis=0, concat_axis=0, tiled=True)
    return arrived.astype(jnp.float32).sum(axis=0)


def dequant(code, scale):
    return (code.astype(jnp.float32) * jnp.repeat(scale, QB, axis=1)).astype(jnp.bfloat16)


def slot_table(expert_ids):
    onehot = (expert_ids[:, None] == jnp.arange(EXPERTS, dtype=jnp.int32)[None, :]).astype(
        jnp.int32
    )
    before = jnp.cumsum(onehot, axis=0) - onehot
    return jnp.sum(before * onehot, axis=1)


def local(
    tokens, routes, route_weight, gate_code, gate_scale, up_code, up_scale, down_code, down_scale
):
    tok_count = tokens.shape[0]
    feature_width = tokens.shape[1]
    members = lax.axis_size("ep") // EXPERTS
    halves = lax.axis_size("tp")
    expert_ids = routes.reshape(-1)
    slot_rank = slot_table(expert_ids)
    slot_span = CAP // halves
    slot_first = lax.axis_index("tp") * slot_span
    gate_code, gate_scale, up_code, up_scale = (
        lax.all_gather(gate_code, "tp", axis=1, tiled=True),
        lax.all_gather(gate_scale.astype(jnp.bfloat16), "tp", axis=1, tiled=True).astype(
            gate_scale.dtype
        ),
        lax.all_gather(up_code, "tp", axis=1, tiled=True),
        lax.all_gather(up_scale.astype(jnp.bfloat16), "tp", axis=1, tiled=True).astype(
            up_scale.dtype
        ),
    )
    down_code, down_scale = (
        lax.all_gather(down_code, "tp", axis=0, tiled=True),
        lax.all_gather(down_scale.astype(jnp.bfloat16), "tp", axis=0, tiled=True).astype(
            down_scale.dtype
        ),
    )
    local_slot = slot_rank - slot_first
    inside = (local_slot >= 0) & (local_slot < slot_span)
    target = jnp.where(inside, expert_ids * slot_span + local_slot, -1)
    columns = jnp.arange(EXPERTS * slot_span, dtype=jnp.int32)
    picked = (target[None, :] == columns[:, None]).astype(jnp.bfloat16)
    repeated = jnp.repeat(tokens, TOP, axis=0)
    outgoing = jnp.dot(picked, repeated, preferred_element_type=jnp.float32).astype(jnp.bfloat16)
    w_gate = dequant(gate_code, gate_scale)
    w_up = dequant(up_code, up_scale)
    w_down = dequant(down_code, down_scale)
    part_width = feature_width // members
    levels = members.bit_length() - 1
    own_index = lax.axis_index("ep")
    spread_rows = outgoing.reshape(EXPERTS, slot_span, members, part_width).transpose(0, 2, 1, 3)
    spread_rows = spread_rows.reshape(EXPERTS * members, slot_span, part_width)
    arrived = lax.all_to_all(spread_rows, "ep", split_axis=0, concat_axis=0, tiled=True)
    for level in range(levels):
        partner = partner_2(arrived, "ep", level)
        level_bit = own_index // 2**level % 2
        arrived = jnp.where(
            level_bit == 0,
            jnp.concatenate((arrived, partner), axis=2),
            jnp.concatenate((partner, arrived), axis=2),
        )
    row_count = arrived.shape[0] * arrived.shape[1]
    arrived_rows = arrived.reshape(row_count, feature_width)
    gate_act = jnp.dot(arrived_rows, w_gate, preferred_element_type=jnp.float32)
    up_act = jnp.dot(arrived_rows, w_up, preferred_element_type=jnp.float32)
    hidden = (jax.nn.silu(gate_act) * up_act).astype(jnp.bfloat16)
    partial_out = jnp.dot(hidden, w_down, preferred_element_type=jnp.float32)
    partial_out = partial_out.reshape(arrived.shape[0], arrived.shape[1], feature_width)
    for level in reversed(range(levels)):
        half_width = partial_out.shape[2] // 2
        lower = partial_out[:, :, :half_width]
        upper = partial_out[:, :, half_width:]
        level_bit = own_index // 2**level % 2
        keeping = jnp.where(level_bit == 0, lower, upper)
        sending = jnp.where(level_bit == 0, upper, lower)
        partial_out = keeping + partner_2(sending.astype(jnp.bfloat16), "ep", level).astype(
            sending.dtype
        )
    collected = lax.all_to_all(
        partial_out.astype(jnp.bfloat16), "ep", split_axis=0, concat_axis=0, tiled=True
    ).astype(partial_out.dtype)
    summed = collected.reshape(EXPERTS, members, slot_span, part_width).transpose(0, 2, 1, 3)
    summed = summed.reshape(EXPERTS * slot_span, feature_width)
    mixing = jnp.where(target[:, None] == columns[None, :], route_weight.reshape(-1)[:, None], 0.0)
    mixing = mixing.reshape(tok_count, TOP, EXPERTS * slot_span).sum(axis=1)
    mixed = jnp.dot(
        mixing, summed, precision=lax.Precision.HIGHEST, preferred_element_type=jnp.float32
    )
    return summed_on_arrival(mixed.astype(jnp.bfloat16), "tp", 1).astype(jnp.bfloat16)


def solution(mesh):
    placed = (
        P(("rep", "ep"), None),
        P(("rep", "ep"), None),
        P(("rep", "ep"), None),
        P(None, ("ep", "tp")),
        P(None, ("ep", "tp")),
        P(None, ("ep", "tp")),
        P(None, ("ep", "tp")),
        P(("ep", "tp"), None),
        P(("ep", "tp"), None),
    )
    return jax.shard_map(
        local, mesh=mesh, in_specs=placed, out_specs=P(("rep", "ep"), "tp"), check_vma=False
    )
```

profile of v0, /device:TPU:37, one launch (start us, length us, event | category | flops | bytes accessed | tf_op | source)
XLA Modules:
  0.0 694.7 jit_solution(12603601668765160565)
XLA Ops:
  10.2 102.5 %all_to_all.15 = bf16[32,20,384]{2,1,0:T(8,128)(2,1)S(1)} all-to-all(bf16[32,20,384]{2,1,0:T(8,128)(2,1)S(1)} %copy.129), channel_id=1, replica_groups=mesh['rep'=4,'ep'=32,'tp'=2] {'ep'}, dimensions={0} | all-to-all | bytes 983040 | tf_op jit(solution)/shard_map/all_to_all | solution.py:87
  112.9 11.4 %collective-permute-done = bf16[32,20,384]{2,0,1:T(8,128)(2,1)S(1)} collective-permute-done((bf16[32,20,384]{2,0,1:T(8,128)(2,1)S(1)}, bf16[32,20,384]{2,0,1:T(8,128)(2,1)S(1)}, u32[]{:S(2)}, u32[]{:S(2)}) %collective-permute-start) | collective-permute-done | bytes 491552 | tf_op jit(solution)/shard_map/ppermute | solution.py:19
  125.2 45.6 %collective-permute-done.1 = bf16[32,20,768]{2,0,1:T(8,128)(2,1)} collective-permute-done((bf16[32,20,768]{2,0,1:T(8,128)(2,1)S(1)}, bf16[32,20,768]{2,0,1:T(8,128)(2,1)}, u32[]{:S(2)}, u32[]{:S(2)}) %collective-permute-start.1) | collective-permute-done | bytes 983072 | tf_op jit(solution)/shard_map/ppermute | solution.py:19
  175.3 2.1 all-gather
  189.1 3.2 maximum_select_fusion.2
  192.3 154.3 %collective-permute-done.2 = bf16[32,20,1536]{2,0,1:T(8,128)(2,1)} collective-permute-done((bf16[32,20,1536]{2,0,1:T(8,128)(2,1)}, bf16[32,20,1536]{2,0,1:T(8,128)(2,1)}, u32[]{:S(2)}, u32[]{:S(2)}) %collective-permute-start.2) | collective-permute-done | bytes 1966112 | tf_op jit(solution)/shard_map/ppermute | solution.py:19
  346.6 2.6 copy.139
  349.2 2.1 concatenate.51
  351.3 4.5 broadcast_in_dim.40
  355.8 11.3 %fusion.3 = f32[640,1024]{1,0:T(8,128)} fusion(f32[384,8,8,128]{3,2,1,0:T(8,128)S(1)} %bitcast.56, bf16[3072,1024]{1,0:T(8,128)(2,1)} %all-gather.6.cloned.1.call-done, bf16[640,1536]{1,0:T(8,128)(2,1)} %concatenate.51, bf16[640,1536]{1,0:T(8,128)(2,1)} %maximum_select_fusion.2, pred[]{:T(512)S(6)} %eq.73), kind=kOutput, calls=%fused_computation.6 | convolution fusion | flops 4053663744 | bytes 25427968 | tf_op jit(solution)/shard_map/dot_general | solution.py:98
  367.2 4.5 broadcast_in_dim.41
  371.7 12.0 %multiply_convert_fusion = bf16[640,1024]{1,0:T(8,128)(2,1)} fusion(f32[640,1024]{1,0:T(8,128)} %fusion.3, f32[384,8,8,128]{3,2,1,0:T(8,128)S(1)} %bitcast.55, bf16[3072,1024]{1,0:T(8,128)(2,1)} %all-gather.8.cloned.1.call-done, bf16[640,1536]{1,0:T(8,128)(2,1)} %concatenate.51, bf16[640,1536]{1,0:T(8,128)(2,1)} %maximum_select_fusion.2, pred[]{:T(512)S(6)} %eq.73), kind=kOutput, calls=%fused_computation.14 | convolution fusion | flops 4057595904 | bytes 26738688 | tf_op jit(solution)/shard_map/dot_general | solution.py:99
  383.7 4.7 broadcast_in_dim.42
  388.4 8.0 %fusion.7 = f32[640,3072]{1,0:T(8,128)} fusion(bf16[640,1024]{1,0:T(8,128)(2,1)S(1)} %copy-done.1, f32[128,8,24,128]{3,2,1,0:T(8,128)S(1)} %bitcast.54, bf16[1024,3072]{1,0:T(8,128)(2,1)S(1)} %copy-done), kind=kOutput, calls=%fused_computation.8 | convolution fusion | flops 4035969024 | bytes 28049408 | tf_op jit(solution)/shard_map/dot_general | solution.py:101
  396.4 9.1 %reshape.94 = f32[32,20,3072]{2,1,0:T(8,128)} reshape(f32[640,3072]{1,0:T(8,128)} %fusion.7) | data formatting | bytes 15728640 | tf_op jit(solution)/shard_map/reshape | solution.py:102
  405.5 4.6 fusion.15
  410.1 4.2 select_convert_fusion
  414.7 128.5 %collective-permute-done.3 = bf16[32,20,1536]{2,0,1:T(8,128)(2,1)S(1)} collective-permute-done((bf16[32,20,1536]{2,0,1:T(8,128)(2,1)S(1)}, bf16[32,20,1536]{2,0,1:T(8,128)(2,1)S(1)}, u32[]{:S(2)}, u32[]{:S(2)}) %collective-permute-start.3) | collective-permute-done | bytes 1966112 | tf_op jit(solution)/shard_map/ppermute | solution.py:19
  543.2 4.4 convert_add_fusion
  547.9 41.9 %collective-permute-done.4 = bf16[32,20,768]{2,0,1:T(8,128)(2,1)S(1)} collective-permute-done((bf16[32,20,768]{2,0,1:T(8,128)(2,1)S(1)}, bf16[32,20,768]{2,0,1:T(8,128)(2,1)S(1)}, u32[]{:S(2)}, u32[]{:S(2)}) %collective-permute-start.4) | collective-permute-done | bytes 983072 | tf_op jit(solution)/shard_map/ppermute | solution.py:19
  590.5 12.3 %collective-permute-done.5 = bf16[32,20,384]{2,0,1:T(8,128)(2,1)S(1)} collective-permute-done((bf16[32,20,384]{2,0,1:T(8,128)(2,1)S(1)}, bf16[32,20,384]{2,0,1:T(8,128)(2,1)S(1)}, u32[]{:S(2)}, u32[]{:S(2)}) %collective-permute-start.5) | collective-permute-done | bytes 491552 | tf_op jit(solution)/shard_map/ppermute | solution.py:19
  603.9 7.9 %all-to-all-start.1 = ((bf16[32,20,384]{2,1,0:T(8,128)(2,1)}), bf16[32,20,384]{2,1,0:T(8,128)(2,1)S(1)}, u32[]{:S(2)}, u32[]{:S(2)}) async-start(bf16[32,20,384]{2,1,0:T(8,128)(2,1)} %copy.145), calls=%async_computation.1 | async-start | bytes 1179648 | tf_op jit(solution)/shard_map/all_to_all | solution.py:113
  612.2 69.0 %all-to-all-done.1 = bf16[32,20,384]{2,1,0:T(8,128)(2,1)S(1)} async-done(((bf16[32,20,384]{2,1,0:T(8,128)(2,1)}), bf16[32,20,384]{2,1,0:T(8,128)(2,1)S(1)}, u32[]{:S(2)}, u32[]{:S(2)}) %all-to-all-start.1) | async-done | bytes 491552 | tf_op jit(solution)/shard_map/all_to_all | solution.py:113
  681.9 5.1 all_to_all.16
  (80 shorter events, 25.0 us)
Async XLA Ops:
  6.5 1.6 copy-start.6
  6.5 1.9 copy-start.2
  6.6 344.8 %all-gather.6.cloned.1.call-start = ((), (), s32[]{:S(2)}) async-start(), calls=%async_computation.3 | async-start | bytes 9437184 | tf_op jit(solution)/shard_map/all_gather | solution.py:57
  7.3 359.8 %all-gather.8.cloned.1.call-start = ((), (), s32[]{:S(2)}) async-start(), calls=%async_computation.4 | async-start | bytes 9437184 | tf_op jit(solution)/shard_map/all_gather | solution.py:61
  8.1 375.6 %all-gather.10.cloned.1.call-start = ((), (), s32[]{:S(2)}) async-start(), calls=%async_computation.5 | async-start | bytes 9437184 | tf_op jit(solution)/shard_map/all_gather | solution.py:67
  112.8 11.5 %collective-permute-start = (bf16[32,20,384]{2,0,1:T(8,128)(2,1)S(1)}, bf16[32,20,384]{2,0,1:T(8,128)(2,1)S(1)}, u32[]{:S(2)}, u32[]{:S(2)}) collective-permute-start(bf16[32,20,384]{2,0,1:T(8,128)(2,1)S(1)} %copy.130), channel_id=1, source_target_pairs={{0,2},{2,0},{4,6},{6,4},{8,10},{10,8},{12,14},{14,12},{16,18},{18,... | collective-permute-start | bytes 1474568 | tf_op jit(solution)/shard_map/ppermute | solution.py:19
  125.0 45.9 %collective-permute-start.1 = (bf16[32,20,768]{2,0,1:T(8,128)(2,1)S(1)}, bf16[32,20,768]{2,0,1:T(8,128)(2,1)}, u32[]{:S(2)}, u32[]{:S(2)}) collective-permute-start(bf16[32,20,768]{2,0,1:T(8,128)(2,1)S(1)} %copy.134), channel_id=1, source_target_pairs={{0,4},{4,0},{2,6},{6,2},{8,12},{12,8},{10,14},{14,10},{16,20},{20,... | collective-permute-start | bytes 2949128 | tf_op jit(solution)/shard_map/ppermute | solution.py:19
  173.3 2.0 copy-start.3
  173.3 5.7 copy-start.4
  173.3 9.2 %copy-start.5 = (f32[512,24]{0,1:T(8,128)S(1)}, f32[512,24]{0,1:T(8,128)}, u32[]{:S(2)}) copy-start(f32[512,24]{0,1:T(8,128)} %param.17) | copy-start | bytes 147460
  175.3 171.3 %collective-permute-start.2 = (bf16[32,20,1536]{2,0,1:T(8,128)(2,1)}, bf16[32,20,1536]{2,0,1:T(8,128)(2,1)}, u32[]{:S(2)}, u32[]{:S(2)}) collective-permute-start(bf16[32,20,1536]{2,0,1:T(8,128)(2,1)} %copy.138), channel_id=1, source_target_pairs={{0,8},{8,0},{2,10},{10,2},{4,12},{12,4},{6,14},{14,6},{16,24},{24,... | collective-permute-start | bytes 5898248 | tf_op jit(solution)/shard_map/ppermute | solution.py:19
  383.7 4.7 copy-start.1
  383.7 4.7 copy-start
  414.3 128.9 %collective-permute-start.3 = (bf16[32,20,1536]{2,0,1:T(8,128)(2,1)S(1)}, bf16[32,20,1536]{2,0,1:T(8,128)(2,1)S(1)}, u32[]{:S(2)}, u32[]{:S(2)}) collective-permute-start(bf16[32,20,1536]{2,0,1:T(8,128)(2,1)S(1)} %select_convert_fusion), channel_id=1, source_target_pairs={{0,8},{8,0},{2,10},{10,2},{4,12},{12,4},{6,14},{14,6},{16,24},{24,... | collective-permute-start | bytes 5898248 | tf_op jit(solution)/shard_map/ppermute | solution.py:19
  547.7 42.1 %collective-permute-start.4 = (bf16[32,20,768]{2,0,1:T(8,128)(2,1)S(1)}, bf16[32,20,768]{2,0,1:T(8,128)(2,1)S(1)}, u32[]{:S(2)}, u32[]{:S(2)}) collective-permute-start(bf16[32,20,768]{2,0,1:T(8,128)(2,1)S(1)} %select_convert_fusion.1), channel_id=1, source_target_pairs={{0,4},{4,0},{2,6},{6,2},{8,12},{12,8},{10,14},{14,10},{16,20},{20,... | collective-permute-start | bytes 2949128 | tf_op jit(solution)/shard_map/ppermute | solution.py:19
  590.2 21.9 %copy-start.7 = (f32[64,2]{0,1:T(2,128)S(1)}, f32[64,2]{0,1:T(2,128)}, u32[]{:S(2)}) copy-start(f32[64,2]{0,1:T(2,128)} %param.11) | copy-start | bytes 1540
  590.3 12.4 %collective-permute-start.5 = (bf16[32,20,384]{2,0,1:T(8,128)(2,1)S(1)}, bf16[32,20,384]{2,0,1:T(8,128)(2,1)S(1)}, u32[]{:S(2)}, u32[]{:S(2)}) collective-permute-start(bf16[32,20,384]{2,0,1:T(8,128)(2,1)S(1)} %select_convert_fusion.2), channel_id=1, source_target_pairs={{0,2},{2,0},{4,6},{6,4},{8,10},{10,8},{12,14},{14,12},{16,18},{18,... | collective-permute-start | bytes 1474568 | tf_op jit(solution)/shard_map/ppermute | solution.py:19
  603.9 77.4 %all-to-all-start.1 = ((bf16[32,20,384]{2,1,0:T(8,128)(2,1)}), bf16[32,20,384]{2,1,0:T(8,128)(2,1)S(1)}, u32[]{:S(2)}, u32[]{:S(2)}) async-start(bf16[32,20,384]{2,1,0:T(8,128)(2,1)} %copy.145), calls=%async_computation.1 | async-start | bytes 1179648 | tf_op jit(solution)/shard_map/all_to_all | solution.py:113
Sparse Core Ops, SparseCore 0:
  9.2 47.2 all-gather.5
  58.3 34.9 all-gather.7
  125.3 21.8 all-gather.9
where the time goes:
time: 702 us; the launch traced here: 695 us
  waiting for transfers between devices  465 us (66%)
  blocking collectives  113 us (16%)
  local copies, waits for them, and re-layouts  45.3 us (6%)
  matrix products  32.1 us (5%)
  other arithmetic  16.4 us (2%)
  between operations  14 us (2%)
  starting transfers between devices  9.01 us (1%)
    ppermute x6, waiting for transfers between devices, partner_2(): return lax.ppermute(block, axis, route)  394 us
    all_to_all x1, blocking collectives, local(): lax.all_to_all(spread_rows, 'ep', split_axis=0, concat_axis=0, tiled=True)  102 us
    all_to_all x1, waiting for transfers between devices, local(): lax.all_to_all(partial_out.astype(jnp.bfloat16), 'ep', split_axis=0, conc...  69 us
  transfers between devices with their start and end apart: 10, of which 7 were waited for; matrix products, arithmetic and copies ran while one was open for 8% of the time, Pallas kernels for 0%

commit v1 on v0

v1 whole, which is shorter than its diff:
```python
import functools

import jax
import jax.numpy as jnp
from jax import lax
from jax.experimental import pallas as pl
from jax.experimental.pallas import tpu as pltpu
from jax.sharding import PartitionSpec as P

EXPERTS = 4
QB = 128
CHUNKS = 4
MESH = pl.DeviceIdType.MESH


def kernel(
    n,
    tokens, routes, weights, gate_code, gate_scale, up_code, up_scale, down_code, down_scale,
    out,
    rows, part, theirs, sums, w_gate, w_up, w_down, s_gate, s_up, s_down,
    hidden, coef, swap_out, swap_in,
    load_sem, ag_send, ag_recv, cf_send, cf_recv, sw_send, sw_recv, sc_send, sc_recv,
    po_send, po_recv, rs_send, rs_recv, fx_send, fx_recv,
):
    steps = n // 2
    count = rows.shape[1] // 2
    half = count // 2
    width = rows.shape[2]
    span = width // CHUNKS
    units = w_gate.shape[1]
    last = steps - 1

    ep = lax.axis_index("ep")
    tp = lax.axis_index("tp")
    toward = 1 - 2 * tp
    ahead = {"ep": lax.rem(ep + toward + n, n)}
    behind = {"ep": lax.rem(ep - toward + n, n)}
    partner = {"tp": 1 - tp}
    expert = ep // (n // EXPERTS)
    own_half = pl.multiple_of(half * tp, half)
    other_half = pl.multiple_of(half * (1 - tp), half)

    def send(src, dst, send_sem, recv_sem, where):
        return pltpu.make_async_remote_copy(
            src_ref=src, dst_ref=dst, send_sem=send_sem, recv_sem=recv_sem,
            device_id=where, device_id_type=MESH,
        )

    own = rows.at[last, pl.ds(count, count)]

    def gather(k, f):
        cols = pl.ds(f * span, span)
        if isinstance(k, int) and k == 1:
            src = own.at[:, cols]
        else:
            src = rows.at[k - 2, pl.ds(0, count), cols]
        return send(
            src, rows.at[k - 1, pl.ds(0, count), cols],
            ag_send.at[lax.rem(k, 2), f], ag_recv.at[k - 1, f], ahead,
        )

    def gather_half(f):
        cols = pl.ds(f * span, span)
        return send(
            rows.at[last - 1, pl.ds(own_half, half), cols], rows.at[last, pl.ds(0, half), cols],
            ag_send.at[steps % 2, f], ag_recv.at[last, f], ahead,
        )

    def gather_coef(k):
        src = coef.at[last, 1] if isinstance(k, int) and k == 1 else coef.at[k - 2, 0]
        return send(
            src, coef.at[k - 1, 0], cf_send.at[lax.rem(k, 2)], cf_recv.at[k - 1], ahead
        )

    def swap(k):
        return send(
            rows.at[k - 1, pl.ds(0, count)], rows.at[k - 1, pl.ds(count, count)],
            sw_send.at[lax.rem(k, 2)], sw_recv.at[k - 1], partner,
        )

    def swap_half():
        return send(
            rows.at[last, pl.ds(0, half)], rows.at[last, pl.ds(half, half)],
            sw_send.at[steps % 2], sw_recv.at[last], partner,
        )

    def swap_coef(k):
        return send(
            coef.at[k - 1, 0], coef.at[k - 1, 1],
            sc_send.at[lax.rem(k, 2)], sc_recv.at[k - 1], partner,
        )

    def hand(k):
        return send(
            part.at[k - 1, pl.ds(count, count)], theirs.at[k - 1],
            po_send.at[lax.rem(k, 2)], po_recv.at[k - 1], partner,
        )

    def hand_half(q):
        cols = pl.ds(q * (width // 2), width // 2)
        return send(
            part.at[last, pl.ds(half, half), cols], theirs.at[last, pl.ds(0, half), cols],
            po_send.at[2 + q], po_recv.at[last + q], partner,
        )

    def column(f):
        chunk = lax.rem(2 * (1 - tp) + f, CHUNKS)
        return pl.ds(pl.multiple_of(chunk * span, span), span)

    def reduce(j, f):
        return send(
            part.at[last - j, pl.ds(0, count), column(f)], sums.at[j, :, column(f)],
            rs_send.at[lax.rem(j, 2), f], rs_recv.at[j, f], behind,
        )

    def reduce_first(f):
        return send(
            part.at[last, pl.ds(0, half), column(f)],
            sums.at[0, pl.ds(own_half, half), column(f)],
            rs_send.at[0, f], rs_recv.at[0, f], behind,
        )

    def finish(i):
        cols = pl.ds(i * span, span)
        return send(
            swap_out.at[:, cols], swap_in.at[:, cols], fx_send.at[i], fx_recv.at[i], partner
        )

    def when(test, do):
        if isinstance(test, bool):
            if test:
                do()
        else:
            pl.when(test)(do)

    loads = [
        pltpu.make_async_copy(src, dst, load_sem.at[i])
        for i, (src, dst) in enumerate((
            (tokens, own), (gate_scale, s_gate), (gate_code, w_gate), (up_scale, s_up),
            (up_code, w_up), (down_scale, s_down), (down_code, w_down),
        ))
    ]
    for load in loads:
        load.start()

    barrier = pltpu.get_barrier_semaphore()
    for device in (ahead, behind, partner):
        pl.semaphore_signal(barrier, inc=1, device_id=device, device_id_type=MESH)

    names = lax.broadcasted_iota(jnp.int32, (8, count), 0)
    mine = jnp.where(names == routes[0:1, :], weights[0:1, :], 0.0)
    mine += jnp.where(names == routes[1:2, :], weights[1:2, :], 0.0)
    coef[last, 1] = jnp.concatenate((mine, jnp.zeros((8, 128 - count), jnp.float32)), axis=1)
    loads[0].wait()
    pl.semaphore_wait(barrier, 3)

    for f in range(CHUNKS):
        gather(1, f).start()
    gather_coef(1).start()

    def poll(k, f):
        def full():
            gather(k, f).wait_recv()
            if isinstance(k, int):
                if k >= 2:
                    gather(k - 1, f).wait_send()
                gather(k + 1, f).start()
                return

            @pl.when(k < last)
            def _():
                gather(k - 1, f).wait_send()
                gather(k + 1, f).start()

            @pl.when(k == last)
            def _():
                gather(k - 1, f).wait_send()
                gather_half(f).start()

        def weights_too():
            gather_coef(k).wait_recv()

            def onward():
                if not isinstance(k, int) or k >= 2:
                    gather_coef(k - 1).wait_send()
                gather_coef(k + 1).start()

            when(k < steps, onward)

        def across():
            if not isinstance(k, int) or k >= 3:
                swap(k - 2).wait_send()
                swap_coef(k - 2).wait_send()
            swap(k).start()
            swap_coef(k).start()

        def across_half():
            swap(steps - 2).wait_send()
            swap_half().start()

        when(k < steps, full)
        when(k == steps, lambda: gather_half(f).wait_recv())
        if f == 0:
            when(k <= steps, weights_too)
        if f == CHUNKS - 1:
            when(k < steps, across)
            when(k == steps, across_half)

    def dequant(code, scale, base):
        blocks = code.shape[1] // QB
        grid = scale[:, pl.ds(base, QB)]
        if blocks % 8:
            pad = jnp.zeros((8 - blocks % 8, QB), jnp.float32)
            grid = jnp.concatenate((grid, pad), axis=0)
        grid = grid.T
        for b in range(blocks):
            at = (pl.ds(base, QB), pl.ds(b * QB, QB))
            code[at] = (code[at].astype(jnp.float32) * grid[:, b : b + 1]).astype(code.dtype)

    def dequant_piece(m, f):
        code, scale = ((w_gate, s_gate), (w_up, s_up), (w_down, s_down))[m]
        size = code.shape[0] // CHUNKS

        @pl.loop(0, size // QB)
        def _(r):
            dequant(code, scale, pl.multiple_of(f * size + r * QB, QB))

    def arrived(k):
        def full():
            swap(k).wait_recv()
            swap_coef(k).wait_recv()

        when(k < steps, full)
        when(k == steps, lambda: swap_half().wait_recv())

    def factors(k):
        shift = jnp.where(k == steps, half * tp, 0)
        token = lax.broadcasted_iota(jnp.int32, (count, 128), 0)
        lane = lax.broadcasted_iota(jnp.int32, (count, 128), 1)
        line = coef[k - 1, 0, pl.ds(expert, 1), :]
        first = jnp.sum(
            jnp.where(lane == ((token + shift) & (count - 1)), line, 0.0), axis=1, keepdims=True
        )
        line = coef[k - 1, 1, pl.ds(expert, 1), :]
        second = jnp.sum(jnp.where(lane == token, line, 0.0), axis=1, keepdims=True)
        return jnp.concatenate((first, second), axis=0)

    def widen(k, p):
        cols = pl.ds(p * (units // 2), units // 2)
        x = rows[k - 1]
        gate = jnp.dot(x, w_gate[:, cols], preferred_element_type=jnp.float32)
        up = jnp.dot(x, w_up[:, cols], preferred_element_type=jnp.float32)
        small = jnp.exp(-jnp.abs(gate))
        silu = gate * (jnp.where(gate >= 0, 1.0, small) / (1.0 + small))
        hidden[:, cols] = (silu * up * factors(k)).astype(hidden.dtype)

    def narrow(k, q):
        cols = pl.ds(q * (width // 2), width // 2)
        got = jnp.dot(hidden[...], w_down[:, cols], preferred_element_type=jnp.float32)
        part[k - 1, :, cols] = got.astype(part.dtype)
        when(k == steps, lambda: hand_half(q).start())
        if q == 1:

            def whole():
                def free():
                    hand(k - 2).wait_send()

                when(k >= 3, free)
                hand(k).start()

            when(k < steps, whole)

    def pieces(k):
        return [
            lambda: arrived(k),
            functools.partial(widen, k, 0),
            functools.partial(widen, k, 1),
            functools.partial(narrow, k, 0),
            functools.partial(narrow, k, 1),
        ]

    for k in range(1, 4):
        loads[2 * k - 1].wait()
        loads[2 * k].wait()
        for f in range(CHUNKS):
            poll(k, f)
            dequant_piece(k - 1, f)

    @pl.loop(4, 6)
    def _(k):
        todo = pieces(2 * k - 7) + pieces(2 * k - 6)
        poll(k, 0)
        for do in todo[0:3]:
            do()
        poll(k, 1)
        for do in todo[3:5]:
            do()
        poll(k, 2)
        for do in todo[5:8]:
            do()
        poll(k, 3)
        for do in todo[8:10]:
            do()

    @pl.loop(6, steps + 2)
    def _(k):
        ready, *todo = pieces(k - 1)
        for f in range(CHUNKS):
            poll(k, f)
            if f == 0:
                ready()
            todo[f]()

    def wide(ref):
        return ref.astype(jnp.float32)

    for f in range(CHUNKS):
        if f == 0:
            hand_half(0).wait_recv()
            hand_half(1).wait_recv()
        cols = column(f)
        part[last, pl.ds(0, half), cols] = (
            wide(part[last, pl.ds(0, half), cols]) + wide(theirs[last, pl.ds(0, half), cols])
        ).astype(part.dtype)
        reduce_first(f).start()

    hand(last).wait_recv()
    for f in range(CHUNKS):
        cols = column(f)
        at, rest = pl.ds(own_half, half), pl.ds(other_half, half)
        part[last - 1, rest, cols] = (
            wide(part[last - 1, rest, cols]) + wide(theirs[last - 1, rest, cols])
        ).astype(part.dtype)
        reduce_first(f).wait_recv()
        part[last - 1, at, cols] = (
            wide(part[last - 1, at, cols])
            + wide(theirs[last - 1, at, cols])
            + wide(sums[0, at, cols])
        ).astype(part.dtype)
        reduce(1, f).start()

    @pl.loop(2, steps)
    def _(j):
        k = last - j
        hand(k + 1).wait_recv()
        for f in range(CHUNKS):
            cols = column(f)
            base = wide(part[k, pl.ds(0, count), cols]) + wide(theirs[k, :, cols])
            reduce(j - 1, f).wait_recv()
            part[k, pl.ds(0, count), cols] = (base + wide(sums[j - 1, :, cols])).astype(part.dtype)

            @pl.when(j == 2)
            def _():
                reduce_first(f).wait_send()

            @pl.when(j > 2)
            def _():
                reduce(j - 2, f).wait_send()

            reduce(j, f).start()

    for f in range(CHUNKS):
        cols = column(f)
        base = wide(part[last, pl.ds(count, count), cols])
        reduce(last, f).wait_recv()
        total = base + wide(sums[last, :, cols])
        if f < CHUNKS // 2:
            swap_out[:, f * span : (f + 1) * span] = total.astype(swap_out.dtype)
            finish(f).start()
        else:
            i = f - CHUNKS // 2
            at = slice(i * span, (i + 1) * span)
            finish(i).wait_recv()
            out[:, at] = (total + wide(swap_in[:, at])).astype(out.dtype)

    for f in range(CHUNKS):
        gather(last, f).wait_send()
        gather_half(f).wait_send()
        reduce(last - 1, f).wait_send()
        reduce(last, f).wait_send()
    gather_coef(last).wait_send()
    gather_coef(steps).wait_send()
    swap(last).wait_send()
    swap_half().wait_send()
    swap_coef(last - 1).wait_send()
    swap_coef(last).wait_send()
    hand(last - 1).wait_send()
    hand(last).wait_send()
    for q in range(2):
        hand_half(q).wait_send()
        finish(q).wait_send()


def local(
    n, tokens, routes, route_weight, gate_code, gate_scale, up_code, up_scale, down_code, down_scale
):
    steps = n // 2
    count, width = tokens.shape
    units = gate_code.shape[1]
    vmem = pl.BlockSpec(memory_space=pltpu.VMEM)
    far = pl.BlockSpec(memory_space=pl.ANY)
    bf16, f32 = jnp.bfloat16, jnp.float32
    dma = pltpu.SemaphoreType.DMA
    return pl.pallas_call(
        functools.partial(kernel, n),
        out_shape=jax.ShapeDtypeStruct((count, width // 2), bf16),
        in_specs=[far, vmem, vmem, far, far, far, far, far, far],
        out_specs=vmem,
        scratch_shapes=[
            pltpu.VMEM((steps, 2 * count, width), bf16),
            pltpu.VMEM((steps, 2 * count, width), bf16),
            pltpu.VMEM((steps, count, width), bf16),
            pltpu.VMEM((steps, count, width), bf16),
            pltpu.VMEM(gate_code.shape, bf16),
            pltpu.VMEM(up_code.shape, bf16),
            pltpu.VMEM(down_code.shape, bf16),
            pltpu.VMEM(gate_scale.shape[::-1], f32),
            pltpu.VMEM(up_scale.shape[::-1], f32),
            pltpu.VMEM(down_scale.shape[::-1], f32),
            pltpu.VMEM((2 * count, units), bf16),
            pltpu.VMEM((steps, 2, 8, 128), f32),
            pltpu.VMEM((count, width // 2), bf16),
            pltpu.VMEM((count, width // 2), bf16),
            dma((7,)),
            dma((2, CHUNKS)),
            dma((steps, CHUNKS)),
            dma((2,)),
            dma((steps,)),
            dma((2,)),
            dma((steps,)),
            dma((2,)),
            dma((steps,)),
            dma((4,)),
            dma((steps + 1,)),
            dma((2, CHUNKS)),
            dma((steps, CHUNKS)),
            dma((2,)),
            dma((2,)),
        ],
        compiler_params=pltpu.CompilerParams(
            collective_id=0, has_side_effects=True, vmem_limit_bytes=62 << 20
        ),
    )(
        tokens, routes.T, route_weight.T, gate_code, gate_scale.T, up_code, up_scale.T,
        down_code, down_scale.T,
    )


def solution(mesh):
    placed = (
        P(("rep", "ep"), None),
        P(("rep", "ep"), None),
        P(("rep", "ep"), None),
        P(None, ("ep", "tp")),
        P(None, ("ep", "tp")),
        P(None, ("ep", "tp")),
        P(None, ("ep", "tp")),
        P(("ep", "tp"), None),
        P(("ep", "tp"), None),
    )
    return jax.shard_map(
        functools.partial(local, mesh.shape["ep"]),
        mesh=mesh,
        in_specs=placed,
        out_specs=P(("rep", "ep"), "tp"),
        check_vma=False,
    )
```

time: 702 us -> 177 us (0.25); the launches traced: 695 us -> 177 us
  waiting for transfers between devices: 465 us -> 0 us
  Pallas kernels: 0 us -> 176 us
  blocking collectives: 113 us -> 0 us
  local copies, waits for them, and re-layouts: 45.3 us -> 1.62 us
  matrix products: 32.1 us -> 0 us
  other arithmetic: 16.4 us -> 0 us
  between operations: 14 us -> 0.01 us
  starting transfers between devices: 9.01 us -> 0 us
    ppermute x6 -> x0, waiting for transfers between devices: 394 us -> none  [partner_2(): return lax.ppermute(block, axis, route)]
    pallas_call x0 -> x1, Pallas kernels: none -> 176 us  [local(): pl.pallas_call(functools.partial(kernel, n), out_shape=jax.ShapeDtypeStru...]
    all_to_all x2 -> x0, blocking collectives: 108 us -> none  [the longest x1 102 us: local(): lax.all_to_all(spread_rows, 'ep', split_axis=0, concat_axis=0, tiled=True)]
    all_to_all x1 -> x0, waiting for transfers between devices: 69 us -> none  [local(): lax.all_to_all(partial_out.astype(jnp.bfloat16), 'ep', split_axis=0, conc...]
    dot_general x5 -> x0, matrix products: 32.1 us -> none  [the longest x1 12 us: local(): up_act = jnp.dot(arrived_rows, w_up, preferred_element_type=jnp.float32)]
    broadcast_in_dim x4 -> x0, local copies, waits for them, and re-layouts: 14.1 us -> none  [the longest x3 13.7 us: dequant(): jnp.repeat(scale, QB, axis=1)]
    reshape x6 -> x0, local copies, waits for them, and re-layouts: 9.68 us -> none  [the longest x1 9.08 us: local(): partial_out.reshape(arrived.shape[0], arrived.shape[1], feature_width)]
    all_to_all x1 -> x0, starting transfers between devices: 7.92 us -> none  [local(): lax.all_to_all(partial_out.astype(jnp.bfloat16), 'ep', split_axis=0, conc...]
  transfers between devices with their start and end apart: 10 -> 0, of which waited for: 7 -> 0; matrix products, arithmetic and copies ran while one was open for 8% -> 0% of each run, Pallas kernels for 0% -> 0%
where the time goes in v1:
time: 177 us
  Pallas kernels  176 us (99%)
    pallas_call x1, Pallas kernels, local(): pl.pallas_call(functools.partial(kernel, n), out_shape=jax.ShapeDtypeStru...  176 us

profile of v1, /device:TPU:37, one launch (start us, length us, event | category | flops | bytes accessed | tf_op | source)
XLA Modules:
  0.0 177.3 jit_solution(5744237368312004457)
XLA Ops:
  0.0 175.7 %shard_map.91 = bf16[64,1536]{1,0:T(8,128)(2,1)} custom-call(bf16[64,3072]{1,0:T(8,128)(2,1)} %tokens.1, s32[2,64]{1,0:T(2,128)} %bitcast.8, f32[2,64]{1,0:T(2,128)} %bitcast.9, bf16[3072,512]{1,0:T(8,128)(2,1)} %gate_code.1, f32[4,3072]{1,0:T(4,128)} %bitcast.5, bf16[3072,512]{1,0:T(8,128)(2,1)} %up_code.1, f32[4,3072]{1,0:T(4,128)} %bitcast.6, ...), custom_call_target="tpu_custom_call" | custom-call | tf_op jit(solution)/shard_map/pallas_call | solution.py:404
  175.7 1.6 copy.11

commit v2 on v1

--- a/solution.py
+++ b/solution.py
@@ -9,7 +9,8 @@
 
 EXPERTS = 4
 QB = 128
-CHUNKS = 4
+CHUNKS = 8
+PIECES = 4
 MESH = pl.DeviceIdType.MESH
 
 
@@ -104,7 +105,7 @@
         )
 
     def column(f):
-        chunk = lax.rem(2 * (1 - tp) + f, CHUNKS)
+        chunk = lax.rem(CHUNKS // 2 * (1 - tp) + f, CHUNKS)
         return pl.ds(pl.multiple_of(chunk * span, span), span)
 
     def reduce(j, f):
@@ -205,6 +206,10 @@
         if f == CHUNKS - 1:
             when(k < steps, across)
             when(k == steps, across_half)
+
+    def polls(k, p):
+        for f in range(CHUNKS // PIECES):
+            poll(k, p * (CHUNKS // PIECES) + f)
 
     def dequant(code, scale, base):
         blocks = code.shape[1] // QB
@@ -219,7 +224,7 @@
 
     def dequant_piece(m, f):
         code, scale = ((w_gate, s_gate), (w_up, s_up), (w_down, s_down))[m]
-        size = code.shape[0] // CHUNKS
+        size = code.shape[0] // PIECES
 
         @pl.loop(0, size // QB)
         def _(r):
@@ -282,34 +287,34 @@
     for k in range(1, 4):
         loads[2 * k - 1].wait()
         loads[2 * k].wait()
-        for f in range(CHUNKS):
-            poll(k, f)
-            dequant_piece(k - 1, f)
+        for p in range(PIECES):
+            polls(k, p)
+            dequant_piece(k - 1, p)
 
     @pl.loop(4, 6)
     def _(k):
         todo = pieces(2 * k - 7) + pieces(2 * k - 6)
-        poll(k, 0)
+        polls(k, 0)
         for do in todo[0:3]:
             do()
-        poll(k, 1)
+        polls(k, 1)
         for do in todo[3:5]:
             do()
-        poll(k, 2)
+        polls(k, 2)
         for do in todo[5:8]:
             do()
-        poll(k, 3)
+        polls(k, 3)
         for do in todo[8:10]:
             do()
 
     @pl.loop(6, steps + 2)
     def _(k):
         ready, *todo = pieces(k - 1)
-        for f in range(CHUNKS):
-            poll(k, f)
-            if f == 0:
+        for p in range(PIECES):
+            polls(k, p)
+            if p == 0:
                 ready()
-            todo[f]()
+            todo[p]()
 
     def wide(ref):
         return ref.astype(jnp.float32)
@@ -388,7 +393,8 @@
     hand(last).wait_send()
     for q in range(2):
         hand_half(q).wait_send()
-        finish(q).wait_send()
+    for i in range(CHUNKS // 2):
+        finish(i).wait_send()
 
 
 def local(
@@ -434,8 +440,8 @@
             dma((steps + 1,)),
             dma((2, CHUNKS)),
             dma((steps, CHUNKS)),
-            dma((2,)),
-            dma((2,)),
+            dma((CHUNKS // 2,)),
+            dma((CHUNKS // 2,)),
         ],
         compiler_params=pltpu.CompilerParams(
             collective_id=0, has_side_effects=True, vmem_limit_bytes=62 << 20

time: 177 us -> 178 us (level)
  no operation moved by 1% of the time
where the time goes in v2:
time: 178 us
  Pallas kernels  177 us (99%)
    pallas_call x1, Pallas kernels, local(): pl.pallas_call(functools.partial(kernel, n), out_shape=jax.ShapeDtypeStru...  177 us

profile of v2, /device:TPU:37, one launch (start us, length us, event | category | flops | bytes accessed | tf_op | source)
XLA Modules:
  0.0 178.3 jit_solution(9970149859744183009)
XLA Ops:
  0.0 176.7 %shard_map.91 = bf16[64,1536]{1,0:T(8,128)(2,1)} custom-call(bf16[64,3072]{1,0:T(8,128)(2,1)} %tokens.1, s32[2,64]{1,0:T(2,128)} %bitcast.8, f32[2,64]{1,0:T(2,128)} %bitcast.9, bf16[3072,512]{1,0:T(8,128)(2,1)} %gate_code.1, f32[4,3072]{1,0:T(4,128)} %bitcast.5, bf16[3072,512]{1,0:T(8,128)(2,1)} %up_code.1, f32[4,3072]{1,0:T(4,128)} %bitcast.6, ...), custom_call_target="tpu_custom_call" | custom-call | tf_op jit(solution)/shard_map/pallas_call | solution.py:410
  176.7 1.6 copy.11

commit v3 on v2

--- a/solution.py
+++ b/solution.py
@@ -19,9 +19,9 @@
     tokens, routes, weights, gate_code, gate_scale, up_code, up_scale, down_code, down_scale,
     out,
     rows, part, theirs, sums, w_gate, w_up, w_down, s_gate, s_up, s_down,
-    hidden, coef, swap_out, swap_in,
+    hidden, coef, swap_out, swap_in, route, weight,
     load_sem, ag_send, ag_recv, cf_send, cf_recv, sw_send, sw_recv, sc_send, sc_recv,
-    po_send, po_recv, rs_send, rs_recv, fx_send, fx_recv,
+    sh_send, sh_recv, po_send, po_recv, rs_send, rs_recv, fx_send, fx_recv,
 ):
     steps = n // 2
     count = rows.shape[1] // 2
@@ -79,10 +79,11 @@
             sw_send.at[lax.rem(k, 2)], sw_recv.at[k - 1], partner,
         )
 
-    def swap_half():
-        return send(
-            rows.at[last, pl.ds(0, half)], rows.at[last, pl.ds(half, half)],
-            sw_send.at[steps % 2], sw_recv.at[last], partner,
+    def swap_half(f):
+        cols = pl.ds(f * span, span)
+        return send(
+            rows.at[last, pl.ds(0, half), cols], rows.at[last, pl.ds(half, half), cols],
+            sh_send.at[f], sh_recv.at[f], partner,
         )
 
     def swap_coef(k):
@@ -98,7 +99,7 @@
         )
 
     def hand_half(q):
-        cols = pl.ds(q * (width // 2), width // 2)
+        cols = pl.ds(pl.multiple_of(q * (width // 2), width // 2), width // 2)
         return send(
             part.at[last, pl.ds(half, half), cols], theirs.at[last, pl.ds(0, half), cols],
             po_send.at[2 + q], po_recv.at[last + q], partner,
@@ -139,24 +140,28 @@
         for i, (src, dst) in enumerate((
             (tokens, own), (gate_scale, s_gate), (gate_code, w_gate), (up_scale, s_up),
             (up_code, w_up), (down_scale, s_down), (down_code, w_down),
+            (routes, route), (weights, weight),
         ))
     ]
-    for load in loads:
-        load.start()
+    for i in (0, 7, 8):
+        loads[i].start()
 
     barrier = pltpu.get_barrier_semaphore()
     for device in (ahead, behind, partner):
         pl.semaphore_signal(barrier, inc=1, device_id=device, device_id_type=MESH)
-
+    pl.semaphore_wait(barrier, 3)
+    loads[0].wait()
+    for f in range(CHUNKS):
+        gather(1, f).start()
+
+    for load in loads[1:7]:
+        load.start()
+    loads[7].wait()
+    loads[8].wait()
     names = lax.broadcasted_iota(jnp.int32, (8, count), 0)
-    mine = jnp.where(names == routes[0:1, :], weights[0:1, :], 0.0)
-    mine += jnp.where(names == routes[1:2, :], weights[1:2, :], 0.0)
+    mine = jnp.where(names == route[0:1, :], weight[0:1, :], 0.0)
+    mine += jnp.where(names == route[1:2, :], weight[1:2, :], 0.0)
     coef[last, 1] = jnp.concatenate((mine, jnp.zeros((8, 128 - count), jnp.float32)), axis=1)
-    loads[0].wait()
-    pl.semaphore_wait(barrier, 3)
-
-    for f in range(CHUNKS):
-        gather(1, f).start()
     gather_coef(1).start()
 
     def poll(k, f):
@@ -178,6 +183,10 @@
                 gather(k - 1, f).wait_send()
                 gather_half(f).start()
 
+        def half_too():
+            gather_half(f).wait_recv()
+            swap_half(f).start()
+
         def weights_too():
             gather_coef(k).wait_recv()
 
@@ -195,17 +204,11 @@
             swap(k).start()
             swap_coef(k).start()
 
-        def across_half():
-            swap(steps - 2).wait_send()
-            swap_half().start()
-
         when(k < steps, full)
-        when(k == steps, lambda: gather_half(f).wait_recv())
-        if f == 0:
-            when(k <= steps, weights_too)
+        when(k == steps, half_too)
         if f == CHUNKS - 1:
+            weights_too()
             when(k < steps, across)
-            when(k == steps, across_half)
 
     def polls(k, p):
         for f in range(CHUNKS // PIECES):
@@ -231,57 +234,54 @@
             dequant(code, scale, pl.multiple_of(f * size + r * QB, QB))
 
     def arrived(k):
-        def full():
-            swap(k).wait_recv()
-            swap_coef(k).wait_recv()
-
-        when(k < steps, full)
-        when(k == steps, lambda: swap_half().wait_recv())
-
-    def factors(k):
-        shift = jnp.where(k == steps, half * tp, 0)
+        swap(k).wait_recv()
+        swap_coef(k).wait_recv()
+
+    def factors(line, shift):
         token = lax.broadcasted_iota(jnp.int32, (count, 128), 0)
         lane = lax.broadcasted_iota(jnp.int32, (count, 128), 1)
-        line = coef[k - 1, 0, pl.ds(expert, 1), :]
-        first = jnp.sum(
+        return jnp.sum(
             jnp.where(lane == ((token + shift) & (count - 1)), line, 0.0), axis=1, keepdims=True
         )
-        line = coef[k - 1, 1, pl.ds(expert, 1), :]
-        second = jnp.sum(jnp.where(lane == token, line, 0.0), axis=1, keepdims=True)
-        return jnp.concatenate((first, second), axis=0)
-
-    def widen(k, p):
+
+    def line(k, side):
+        return coef[k - 1, side, pl.ds(expert, 1), :]
+
+    def widen(k, p, low, size, factor):
         cols = pl.ds(p * (units // 2), units // 2)
-        x = rows[k - 1]
+        x = rows[k - 1, low : low + size]
         gate = jnp.dot(x, w_gate[:, cols], preferred_element_type=jnp.float32)
         up = jnp.dot(x, w_up[:, cols], preferred_element_type=jnp.float32)
         small = jnp.exp(-jnp.abs(gate))
         silu = gate * (jnp.where(gate >= 0, 1.0, small) / (1.0 + small))
-        hidden[:, cols] = (silu * up * factors(k)).astype(hidden.dtype)
-
-    def narrow(k, q):
-        cols = pl.ds(q * (width // 2), width // 2)
-        got = jnp.dot(hidden[...], w_down[:, cols], preferred_element_type=jnp.float32)
-        part[k - 1, :, cols] = got.astype(part.dtype)
-        when(k == steps, lambda: hand_half(q).start())
-        if q == 1:
-
-            def whole():
-                def free():
-                    hand(k - 2).wait_send()
-
-                when(k >= 3, free)
-                hand(k).start()
-
-            when(k < steps, whole)
+        hidden[low : low + size, cols] = (silu * up * factor()).astype(hidden.dtype)
+
+    def narrow(k, q, low, size):
+        cols = pl.ds(pl.multiple_of(q * (width // 2), width // 2), width // 2)
+        got = jnp.dot(
+            hidden[low : low + size], w_down[:, cols], preferred_element_type=jnp.float32
+        )
+        part[k - 1, low : low + size, cols] = got.astype(part.dtype)
 
     def pieces(k):
+        def both():
+            return jnp.concatenate((factors(line(k, 0), 0), factors(line(k, 1), 0)), axis=0)
+
+        def give():
+            narrow(k, 1, 0, 2 * count)
+
+            @pl.when(k >= 3)
+            def _():
+                hand(k - 2).wait_send()
+
+            hand(k).start()
+
         return [
             lambda: arrived(k),
-            functools.partial(widen, k, 0),
-            functools.partial(widen, k, 1),
-            functools.partial(narrow, k, 0),
-            functools.partial(narrow, k, 1),
+            lambda: widen(k, 0, 0, 2 * count, both),
+            lambda: widen(k, 1, 0, 2 * count, both),
+            lambda: narrow(k, 0, 0, 2 * count),
+            give,
         ]
 
     for k in range(1, 4):
@@ -307,7 +307,7 @@
         for do in todo[8:10]:
             do()
 
-    @pl.loop(6, steps + 2)
+    @pl.loop(6, steps + 1)
     def _(k):
         ready, *todo = pieces(k - 1)
         for p in range(PIECES):
@@ -320,14 +320,26 @@
         return ref.astype(jnp.float32)
 
     for f in range(CHUNKS):
+        swap_half(f).wait_recv()
+    for p in range(2):
+        widen(steps, p, 0, count, lambda: factors(line(steps, 0), half * tp))
+    for q in (tp, 1 - tp):
+        narrow(steps, q, 0, count)
+        hand_half(q).start()
+    for f in range(CHUNKS):
         if f == 0:
-            hand_half(0).wait_recv()
-            hand_half(1).wait_recv()
+            hand_half(1 - tp).wait_recv()
+        if f == CHUNKS // 2:
+            hand_half(tp).wait_recv()
         cols = column(f)
         part[last, pl.ds(0, half), cols] = (
             wide(part[last, pl.ds(0, half), cols]) + wide(theirs[last, pl.ds(0, half), cols])
         ).astype(part.dtype)
         reduce_first(f).start()
+    for p in range(2):
+        widen(steps, p, count, count, lambda: factors(line(steps, 1), 0))
+    for q in range(2):
+        narrow(steps, q, count, count)
 
     hand(last).wait_recv()
     for f in range(CHUNKS):
@@ -383,10 +395,11 @@
         gather_half(f).wait_send()
         reduce(last - 1, f).wait_send()
         reduce(last, f).wait_send()
+        swap_half(f).wait_send()
     gather_coef(last).wait_send()
     gather_coef(steps).wait_send()
     swap(last).wait_send()
-    swap_half().wait_send()
+    swap(last - 1).wait_send()
     swap_coef(last - 1).wait_send()
     swap_coef(last).wait_send()
     hand(last - 1).wait_send()
@@ -410,7 +423,7 @@
     return pl.pallas_call(
         functools.partial(kernel, n),
         out_shape=jax.ShapeDtypeStruct((count, width // 2), bf16),
-        in_specs=[far, vmem, vmem, far, far, far, far, far, far],
+        in_specs=[far] * 9,
         out_specs=vmem,
         scratch_shapes=[
             pltpu.VMEM((steps, 2 * count, width), bf16),
@@ -427,7 +440,9 @@
             pltpu.VMEM((steps, 2, 8, 128), f32),
             pltpu.VMEM((count, width // 2), bf16),
             pltpu.VMEM((count, width // 2), bf16),
-            dma((7,)),
+            pltpu.VMEM((2, count), jnp.int32),
+            pltpu.VMEM((2, count), f32),
+            dma((9,)),
             dma((2, CHUNKS)),
             dma((steps, CHUNKS)),
             dma((2,)),
@@ -436,6 +451,8 @@
             dma((steps,)),
             dma((2,)),
             dma((steps,)),
+            dma((CHUNKS,)),
+            dma((CHUNKS,)),
             dma((4,)),
             dma((steps + 1,)),
             dma((2, CHUNKS)),

time: 178 us -> 174 us (0.978)
  Pallas kernels: 177 us -> 172 us
    pallas_call x1, Pallas kernels: 177 us -> 172 us  [local(): pl.pallas_call(functools.partial(kernel, n), out_shape=jax.ShapeDtypeStru...]
where the time goes in v3:
time: 174 us
  Pallas kernels  172 us (99%)
    pallas_call x1, Pallas kernels, local(): pl.pallas_call(functools.partial(kernel, n), out_shape=jax.ShapeDtypeStru...  172 us

profile of v3, /device:TPU:37, one launch (start us, length us, event | category | flops | bytes accessed | tf_op | source)
XLA Modules:
  0.0 174.0 jit_solution(17062413799374953047)
XLA Ops:
  0.0 172.4 %shard_map.91 = bf16[64,1536]{1,0:T(8,128)(2,1)} custom-call(bf16[64,3072]{1,0:T(8,128)(2,1)} %tokens.1, s32[2,64]{1,0:T(2,128)} %bitcast.8, f32[2,64]{1,0:T(2,128)} %bitcast.9, bf16[3072,512]{1,0:T(8,128)(2,1)} %gate_code.1, f32[4,3072]{1,0:T(4,128)} %bitcast.5, bf16[3072,512]{1,0:T(8,128)(2,1)} %up_code.1, f32[4,3072]{1,0:T(4,128)} %bitcast.6, ...), custom_call_target="tpu_custom_call" | custom-call | tf_op jit(solution)/shard_map/pallas_call | solution.py:423
  172.4 1.6 copy.11

commit v4 on v3

--- a/solution.py
+++ b/solution.py
@@ -19,7 +19,7 @@
     tokens, routes, weights, gate_code, gate_scale, up_code, up_scale, down_code, down_scale,
     out,
     rows, part, theirs, sums, w_gate, w_up, w_down, s_gate, s_up, s_down,
-    hidden, coef, swap_out, swap_in, route, weight,
+    hidden, coef, swap_out, swap_in, route, weight, gate_sum, up_sum,
     load_sem, ag_send, ag_recv, cf_send, cf_recv, sw_send, sw_recv, sc_send, sc_recv,
     sh_send, sh_recv, po_send, po_recv, rs_send, rs_recv, fx_send, fx_recv,
 ):
@@ -158,10 +158,13 @@
         load.start()
     loads[7].wait()
     loads[8].wait()
-    names = lax.broadcasted_iota(jnp.int32, (8, count), 0)
-    mine = jnp.where(names == route[0:1, :], weight[0:1, :], 0.0)
-    mine += jnp.where(names == route[1:2, :], weight[1:2, :], 0.0)
-    coef[last, 1] = jnp.concatenate((mine, jnp.zeros((8, 128 - count), jnp.float32)), axis=1)
+    twice = [jnp.concatenate((route[i : i + 1, :],) * 2, axis=1) for i in range(2)]
+    shares = [jnp.concatenate((weight[i : i + 1, :],) * 2, axis=1) for i in range(2)]
+    names = 2 * lax.broadcasted_iota(jnp.int32, (2, 2 * count), 0)
+    names += jnp.where(lax.broadcasted_iota(jnp.int32, (2, 2 * count), 1) >= count, 1, 0)
+    coef[last, 1] = jnp.where(names == twice[0], shares[0], 0.0) + jnp.where(
+        names == twice[1], shares[1], 0.0
+    )
     gather_coef(1).start()
 
     def poll(k, f):
@@ -241,20 +244,24 @@
         token = lax.broadcasted_iota(jnp.int32, (count, 128), 0)
         lane = lax.broadcasted_iota(jnp.int32, (count, 128), 1)
         return jnp.sum(
-            jnp.where(lane == ((token + shift) & (count - 1)), line, 0.0), axis=1, keepdims=True
+            jnp.where(lane == ((token + shift) & (count - 1)) + count * lax.rem(expert, 2), line, 0.0),
+            axis=1,
+            keepdims=True,
         )
 
     def line(k, side):
-        return coef[k - 1, side, pl.ds(expert, 1), :]
+        return coef[k - 1, side, pl.ds(expert // 2, 1), :]
+
+    def gated(gate, up):
+        small = jnp.exp(-jnp.abs(gate))
+        return gate * (jnp.where(gate >= 0, 1.0, small) / (1.0 + small)) * up
 
     def widen(k, p, low, size, factor):
         cols = pl.ds(p * (units // 2), units // 2)
         x = rows[k - 1, low : low + size]
         gate = jnp.dot(x, w_gate[:, cols], preferred_element_type=jnp.float32)
         up = jnp.dot(x, w_up[:, cols], preferred_element_type=jnp.float32)
-        small = jnp.exp(-jnp.abs(gate))
-        silu = gate * (jnp.where(gate >= 0, 1.0, small) / (1.0 + small))
-        hidden[low : low + size, cols] = (silu * up * factor()).astype(hidden.dtype)
+        hidden[low : low + size, cols] = (gated(gate, up) * factor()).astype(hidden.dtype)
 
     def narrow(k, q, low, size):
         cols = pl.ds(pl.multiple_of(q * (width // 2), width // 2), width // 2)
@@ -319,10 +326,17 @@
     def wide(ref):
         return ref.astype(jnp.float32)
 
-    for f in range(CHUNKS):
-        swap_half(f).wait_recv()
-    for p in range(2):
-        widen(steps, p, 0, count, lambda: factors(line(steps, 0), half * tp))
+    for g in range(PIECES):
+        for f in range(CHUNKS // PIECES):
+            swap_half(g * (CHUNKS // PIECES) + f).wait_recv()
+        depth = slice(g * (width // PIECES), (g + 1) * (width // PIECES))
+        x = rows[last, 0:count, depth]
+        for acc, w in ((gate_sum, w_gate), (up_sum, w_up)):
+            got = jnp.dot(x, w[depth, :], preferred_element_type=jnp.float32)
+            acc[...] = got if g == 0 else acc[...] + got
+    hidden[0:count, :] = (
+        gated(gate_sum[...], up_sum[...]) * factors(line(steps, 0), half * tp)
+    ).astype(hidden.dtype)
     for q in (tp, 1 - tp):
         narrow(steps, q, 0, count)
         hand_half(q).start()
@@ -437,11 +451,13 @@
             pltpu.VMEM(up_scale.shape[::-1], f32),
             pltpu.VMEM(down_scale.shape[::-1], f32),
             pltpu.VMEM((2 * count, units), bf16),
-            pltpu.VMEM((steps, 2, 8, 128), f32),
+            pltpu.VMEM((steps, 2, 2, 2 * count), f32),
             pltpu.VMEM((count, width // 2), bf16),
             pltpu.VMEM((count, width // 2), bf16),
             pltpu.VMEM((2, count), jnp.int32),
             pltpu.VMEM((2, count), f32),
+            pltpu.VMEM((count, units), f32),
+            pltpu.VMEM((count, units), f32),
             dma((9,)),
             dma((2, CHUNKS)),
             dma((steps, CHUNKS)),

time: 174 us -> 174 us (level)
  no operation moved by 1% of the time
where the time goes in v4:
time: 174 us
  Pallas kernels  172 us (99%)
    pallas_call x1, Pallas kernels, local(): pl.pallas_call(functools.partial(kernel, n), out_shape=jax.ShapeDtypeStru...  172 us

profile of v4, /device:TPU:37, one launch (start us, length us, event | category | flops | bytes accessed | tf_op | source)
XLA Modules:
  0.0 173.6 jit_solution(1682233578295919570)
XLA Ops:
  0.0 171.9 %shard_map.91 = bf16[64,1536]{1,0:T(8,128)(2,1)} custom-call(bf16[64,3072]{1,0:T(8,128)(2,1)} %tokens.1, s32[2,64]{1,0:T(2,128)} %bitcast.8, f32[2,64]{1,0:T(2,128)} %bitcast.9, bf16[3072,512]{1,0:T(8,128)(2,1)} %gate_code.1, f32[4,3072]{1,0:T(4,128)} %bitcast.5, bf16[3072,512]{1,0:T(8,128)(2,1)} %up_code.1, f32[4,3072]{1,0:T(4,128)} %bitcast.6, ...), custom_call_target="tpu_custom_call" | custom-call | tf_op jit(solution)/shard_map/pallas_call | solution.py:437
  172.0 1.6 copy.11
